TPU v7x, 32 devices: a whole 2x2x4 slice. The times are simulated.
32 devices in a mesh: ba: 8 (over y, x, core), col: 4 (over z).
Axes of the slice: x: 2, y: 2, z: 4, core: 2. Of those that a mesh axis runs over, the one named last changes fastest.
Arguments:
- r_pairs: bfloat16 [1, 3, 512, 512], replicated, may hold values from -6 to 6
- w_tiles: bfloat16 [1, 3, 512, 512, 512], P(None, None, 'ba', 'col'), may hold values from -0.375 to 0.375
- virt_energy: float32 [512], replicated, may hold values from 0.3 to 3
- energy_shift: float32 [1], replicated, may hold values from -14 to -8
Outputs:
- sigma: float32 [1, 3, 512, 512], P(None, None, 'ba', 'col')
All inputs are finite; a program needn't handle non-finite values.
Results may differ from a plain program's by a relative error of at most 0.00077.
Values may be sent and summed in bfloat16 or wider, within the bound.
A program may use at most 128 MiB of HBM per device.

v0:
```python
import functools

import jax
import jax.numpy as jnp
from jax import lax
from jax.experimental import pallas as pl
from jax.experimental.pallas import tpu as pltpu
from jax.sharding import PartitionSpec as P

MESH = pl.DeviceIdType.MESH
CHUNKS = 8
GROUP = 16
SLOTS = 4
LANES = 128
BF16, F32 = jnp.bfloat16, jnp.float32


def whole_kernel(nb, nc, chunks, *refs):
    cube, w_tiles, base_a, energy_b, energy_c, sigma = refs[:6]
    slab, turned, summed, home, combined, w_slots, total = refs[6:13]
    halved, dealt, spread_out = refs[13:-8], refs[-8], refs[-7]
    out_sems, in_sems, own_sems, w_sems, send_sems, got_sems = refs[-6:]
    rows, bw, cw = slab.shape[2:]
    width = nb * bw
    ratio = nb // nc
    bits = nb.bit_length() - 1
    b_me, c_me = lax.axis_index("ba"), lax.axis_index("col")
    barrier = pltpu.get_barrier_semaphore()
    for step in range(1, nb):
        pl.semaphore_signal(barrier, inc=1, device_id=(b_me ^ step, c_me), device_id_type=MESH)
    for step in range(1, nc):
        pl.semaphore_signal(barrier, inc=1, device_id=(b_me, c_me ^ step), device_id_type=MESH)
    pl.semaphore_wait(barrier, nb + nc - 2)

    def spread(chunk):
        for step in range(1, nb):
            pltpu.make_async_remote_copy(
                src_ref=cube.at[b_me ^ step, chunk],
                dst_ref=slab.at[chunk, b_me],
                send_sem=out_sems.at[0, chunk],
                recv_sem=in_sems.at[0, chunk],
                device_id=(b_me ^ step, c_me),
                device_id_type=MESH,
            ).start()

    def own_slab(chunk):
        return pltpu.make_async_copy(cube.at[b_me, chunk], slab.at[chunk, b_me], own_sems.at[0, chunk])

    def own_turned(chunk):
        return pltpu.make_async_copy(
            slab.at[chunk, pl.ds(c_me * ratio, ratio)], turned.at[chunk, c_me], own_sems.at[1, chunk]
        )

    def own_home(chunk):
        return pltpu.make_async_copy(summed.at[chunk, b_me], home.at[chunk, b_me], own_sems.at[2, chunk])

    def turn(chunk):
        for step in range(1, nc):
            level = c_me ^ step
            pltpu.make_async_remote_copy(
                src_ref=slab.at[chunk, pl.ds(level * ratio, ratio)],
                dst_ref=turned.at[chunk, c_me],
                send_sem=out_sems.at[1, chunk],
                recv_sem=in_sems.at[1, chunk],
                device_id=(b_me, level),
                device_id_type=MESH,
            ).start()

    def back(chunk):
        for step in range(1, nb):
            pltpu.make_async_remote_copy(
                src_ref=summed.at[chunk, b_me ^ step],
                dst_ref=home.at[chunk, b_me],
                send_sem=out_sems.at[2, chunk],
                recv_sem=in_sems.at[2, chunk],
                device_id=(b_me ^ step, c_me),
                device_id_type=MESH,
            ).start()

    buffers = (slab, turned, home)
    peers = (nb - 1, nc - 1, nb - 1)

    def arrived(kind, chunk):
        whole = buffers[kind].at[chunk, pl.ds(0, peers[kind])]
        pltpu.make_async_copy(whole, whole, in_sems.at[kind, chunk]).wait()

    def left(kind, chunk):
        whole = buffers[kind].at[chunk, pl.ds(0, peers[kind])]
        pltpu.make_async_copy(whole, whole, out_sems.at[kind, chunk]).wait()

    def add(chunk):
        @pl.loop(0, rows)
        def _(row):
            for level in range(nc):
                other = jnp.concatenate([turned[chunk, level, part, row] for part in range(ratio)], 0)
                flipped = other.astype(F32).T
                for part in range(ratio):
                    block = level * ratio + part
                    kept = slab[chunk, block, row].astype(F32)
                    summed[chunk, block, row] = (kept + flipped[part * bw : (part + 1) * bw]).astype(BF16)

    per = GROUP // rows
    steps = bw // GROUP
    row_c = energy_c[...]
    pack = max(1, LANES // cw)

    def gathered(ref, index, block, inner):
        return jnp.concatenate([ref[index * per + n, block, :, inner, :] for n in range(per)], 0)

    def combine(a_step, b_step, block):
        a_inner = pl.ds(pl.multiple_of(a_step * GROUP, GROUP), GROUP)
        b_inner = pl.ds(pl.multiple_of(b_step * GROUP, GROUP), GROUP)
        mine = gathered(summed, b_step, block, a_inner).astype(F32)
        theirs = gathered(home, a_step, block, b_inner).astype(F32)
        both = mine + jnp.swapaxes(theirs, 0, 1)
        a_rows = pl.ds(pl.multiple_of(block * bw + a_step * GROUP, GROUP), GROUP)
        base = base_a[a_rows, :]
        for b in range(0, GROUP, pack):
            place = b_step * GROUP + b
            entries = [both[b + n] / (base - energy_b[place + n] - row_c) for n in range(pack)]
            lanes = pl.ds(pl.multiple_of(place * cw, pack * cw), pack * cw)
            combined[a_rows, lanes] = jnp.concatenate(entries, 1).astype(BF16)

    def widen(step):
        for n in range(per):
            arrived(2, step * per + n)
            own_home(step * per + n).wait()

        @pl.loop(0, (2 * step + 1) * nb)
        def _(place):
            cell, block = place // nb, place % nb
            a_step = jnp.where(cell <= step, step, cell - step - 1)
            b_step = jnp.where(cell <= step, cell, step)
            combine(a_step, b_step, block)

    part_width = width // 2
    units = 6
    tiles = bw // GROUP
    depth = GROUP * cw

    def fetch(index):
        unit, tile = index // tiles, index % tiles
        slot = index % SLOTS
        return pltpu.make_async_copy(
            w_tiles.at[
                0,
                unit // 2,
                pl.ds(tile * GROUP, GROUP),
                :,
                pl.ds(pl.multiple_of((unit % 2) * part_width, part_width), part_width),
            ],
            w_slots.at[slot],
            w_sems.at[slot],
        )

    def product(unit):
        where = [unit // 2] + [slice(None)] * bits + [slice(None), pl.ds((unit % 2) * part_width, part_width)]

        @pl.loop(0, tiles)
        def _(tile):
            index = unit * tiles + tile
            fetch(index).wait()
            entries = combined[:, pl.ds(pl.multiple_of(tile * depth, depth), depth)]
            piece = jnp.dot(
                entries, w_slots[index % SLOTS].reshape(depth, part_width), preferred_element_type=F32
            ).reshape([2] * bits + [bw, part_width])

            @pl.when(tile == 0)
            def _():
                total[tuple(where)] = piece

            @pl.when(tile > 0)
            def _():
                total[tuple(where)] = total[tuple(where)] + piece

            @pl.when(index + SLOTS < units * tiles)
            def _():
                fetch(index + SLOTS).start()

    def bit(place):
        return (b_me // (1 << place)) % 2

    def order(unit):
        return list(range(bits)) if unit % 2 == 0 else [0] + list(range(1, bits))[::-1]

    def region(unit, fixed):
        lanes = pl.ds((unit % 2) * part_width, part_width)
        picks = [fixed.get(place, slice(None)) for place in range(bits)[::-1]]
        return tuple([unit // 2] + picks + [slice(None), lanes])

    def halving(unit, stage):
        done = order(unit)[:stage]
        place = order(unit)[stage]
        fixed = {n: bit(n) for n in done}
        fixed[place] = 1 - bit(place)
        return pltpu.make_async_remote_copy(
            src_ref=total.at[region(unit, fixed)],
            dst_ref=halved[stage].at[unit],
            send_sem=send_sems.at[unit, stage],
            recv_sem=got_sems.at[unit, stage],
            device_id=(b_me ^ (1 << place), c_me),
            device_id_type=MESH,
        )

    def halved_add(unit, stage):
        halving(unit, stage).wait_recv()
        where = region(unit, {n: bit(n) for n in order(unit)[: stage + 1]})
        total[where] = total[where] + halved[stage][unit]

    levels = nc // 2

    def deal(unit, n):
        level = (unit % 2) * levels + n
        return level, pltpu.make_async_remote_copy(
            src_ref=dealt.at[unit, n],
            dst_ref=spread_out.at[unit // 2, c_me],
            send_sem=send_sems.at[unit, bits + n],
            recv_sem=got_sems.at[unit // 2, bits],
            device_id=(b_me, level),
            device_id_type=MESH,
        )

    def deal_blocks(unit):
        block = total[region(unit, {place: bit(place) for place in range(bits)})]
        for n in range(levels):
            dealt[unit, n] = block[:, n * cw : (n + 1) * cw]

    def deal_start(unit):
        for n in range(levels):
            level, copy = deal(unit, n)
            pl.when(level != c_me)(copy.start)

    def deal_sent(unit):
        for n in range(levels):
            level, copy = deal(unit, n)
            pl.when(level != c_me)(copy.wait_send)

    def finish(unit):
        @pl.when(c_me // levels == unit % 2)
        def _():
            landed = spread_out.at[unit // 2, pl.ds(0, nc - 1)]
            pltpu.make_async_copy(landed, landed, got_sems.at[unit // 2, bits]).wait()
            result = dealt[unit, c_me % levels]
            for step in range(1, nc):
                result = result + spread_out[unit // 2, c_me ^ step]
            sigma[unit // 2] = result

    for index in range(SLOTS):
        fetch(index).start()

    @pl.loop(0, chunks)
    def _(chunk):
        spread(chunk)
        own_slab(chunk).start()

    def settle(chunk):
        arrived(1, chunk)
        own_turned(chunk).wait()
        add(chunk)
        back(chunk)
        own_home(chunk).start()

    for chunk in range(chunks):
        arrived(0, chunk)
        own_slab(chunk).wait()
        turn(chunk)
        own_turned(chunk).start()
        if chunk > 0:
            settle(chunk - 1)
        early = steps - chunks + chunk - 1
        if early >= 0:
            widen(early)
    settle(chunks - 1)
    widen(steps - 1)

    for time in range(units + bits + 1):
        if time < units:
            product(time)
        for stage in range(bits):
            if 0 <= time - stage - 1 < units:
                halved_add(time - stage - 1, stage)
        if 0 <= time - bits < units:
            deal_blocks(time - bits)
        for stage in range(bits):
            if 0 <= time - stage < units:
                halving(time - stage, stage).start()
        if 0 <= time - bits < units:
            deal_start(time - bits)
        if 0 <= time - bits - 1 < units:
            finish(time - bits - 1)
    for unit in range(units):
        for stage in range(bits):
            halving(unit, stage).wait_send()
        deal_sent(unit)

    @pl.loop(0, chunks)
    def _(chunk):
        for kind in range(3):
            left(kind, chunk)


def doubles(cubes, w_tiles, base_a, energy_b, energy_c, nb, nc):
    chunks, rows, bw, cw = cubes.shape[1:]
    width = nb * bw
    bits = nb.bit_length() - 1
    block = (rows, bw, cw)
    vmem = pl.BlockSpec(memory_space=pltpu.VMEM)
    hbm = pl.BlockSpec(memory_space=pl.ANY)
    return pl.pallas_call(
        functools.partial(whole_kernel, nb, nc, chunks),
        out_shape=jax.ShapeDtypeStruct((3, bw, cw), F32),
        in_specs=[hbm, hbm, vmem, pl.BlockSpec(memory_space=pltpu.SMEM), vmem],
        out_specs=vmem,
        scratch_shapes=[
            pltpu.VMEM((chunks, nb) + block, BF16),
            pltpu.VMEM((chunks, nc, nb // nc) + block, BF16),
            pltpu.VMEM((chunks, nb) + block, BF16),
            pltpu.VMEM((chunks, nb) + block, BF16),
            pltpu.VMEM((width, bw * cw), BF16),
            pltpu.VMEM((SLOTS, GROUP, cw, width // 2), BF16),
            pltpu.VMEM((3,) + (2,) * bits + (bw, width), F32),
        ]
        + [pltpu.VMEM((6,) + (2,) * (bits - 1 - stage) + (bw, width // 2), F32) for stage in range(bits)]
        + [
            pltpu.VMEM((6, nc // 2, bw, cw), F32),
            pltpu.VMEM((3, nc, bw, cw), F32),
            pltpu.SemaphoreType.DMA((3, chunks)),
            pltpu.SemaphoreType.DMA((3, chunks)),
            pltpu.SemaphoreType.DMA((3, chunks)),
            pltpu.SemaphoreType.DMA((SLOTS,)),
            pltpu.SemaphoreType.DMA((6, bits + nc // 2)),
            pltpu.SemaphoreType.DMA((6, bits + 1)),
        ],
        compiler_params=pltpu.CompilerParams(
            collective_id=0, has_side_effects=True, vmem_limit_bytes=60 << 20
        ),
    )(cubes, w_tiles, base_a, energy_b, energy_c)


def on_device(r_pairs, w_tiles, virt_energy, energy_shift):
    width = w_tiles.shape[4]
    bw, cw = w_tiles.shape[2], w_tiles.shape[3]
    nb, nc = lax.axis_size("ba"), lax.axis_size("col")
    energy_b = lax.dynamic_slice_in_dim(virt_energy, lax.axis_index("ba") * bw, bw)
    energy_c = lax.dynamic_slice_in_dim(virt_energy, lax.axis_index("col") * cw, cw)
    base_a = jnp.broadcast_to((energy_shift - virt_energy)[:, None], (width, cw))
    flat = w_tiles.reshape(3, bw * cw, width)
    cubes = jnp.einsum("mad,mxd->ax", r_pairs[0], flat, preferred_element_type=F32)
    cubes = cubes.astype(BF16).reshape(nb, CHUNKS, bw // CHUNKS, bw, cw)
    return doubles(cubes, w_tiles, base_a, energy_b, energy_c[None], nb, nc)[None]


def solution(mesh):
    in_specs = (P(), P(None, None, "ba", "col", None), P(), P())
    out_specs = P(None, None, "ba", "col")
    return jax.shard_map(
        on_device, mesh=mesh, in_specs=in_specs, out_specs=out_specs, check_vma=False
    )
```

profile of v0, /device:TPU:0, one launch (start us, length us, event | category | flops | bytes accessed | tf_op | source)
XLA Modules:
  0.0 294.5 jit_solution(18429839017716007707)
XLA Ops:
  0.0 0.0 copy-start
  0.0 1.4 copy-done
  1.4 19.0 %fusion = bf16[64,8,64,128]{3,1,2,0:T(8,128)(2,1)} fusion(bf16[3,8192,512]{2,1,0:T(8,128)(2,1)} %bitcast.19, bf16[1,3,512,512]{3,2,1,0:T(8,128)(2,1)S(1)} %copy-done), kind=kOutput, calls=%fused_computation.1 | convolution fusion | flops 12889096192 | bytes 35127296 | tf_op jit(solution)/shard_map/mad,mxd->ax/dot_general | solution.py:348
  20.4 0.0 copy-start.1
  20.4 9.3 %copy.5 = bf16[64,8,64,128]{3,2,1,0:T(8,128)(2,1)} copy(bf16[64,8,64,128]{3,1,2,0:T(8,128)(2,1)} %fusion) | data formatting | bytes 16777216
  30.4 0.0 copy-done.1
  30.4 0.9 broadcast_in_dim.12.refs_2_
  31.2 0.6 dynamic_slice.6.refs_3_
  31.8 0.6 dynamic-slice_bitcast_fusion.refs_4_
  32.4 260.5 %shard_map.46 = f32[3,64,128]{2,1,0:T(8,128)} custom-call(bf16[8,8,8,64,128]{4,3,2,1,0:T(8,128)(2,1)} %bitcast.18, bf16[1,3,64,128,512]{4,3,2,1,0:T(8,128)(2,1)} %refs_1_.1, f32[512,128]{1,0:T(8,128)} %broadcast_in_dim.12.refs_2_, f32[64]{0:T(128)} %dynamic_slice.6.refs_3_, f32[1,128]{1,0:T(1,128)} %dynamic-slice_bitcast_fusion.refs_4_), custom_call_target="tpu_custom_call" | custom-call | tf_op jit(solution)/shard_map/pallas_call | solution.py:309
  292.9 1.5 copy.8
  (1 shorter events, 0.0 us)
Async XLA Ops:
  0.0 1.4 copy-start
  20.4 10.0 %copy-start.1 = (f32[512]{0:T(512)S(1)}, f32[512]{0:T(512)}, u32[]{:S(2)}) copy-start(f32[512]{0:T(512)} %param.6) | copy-start | bytes 6148
where the time goes:
time: 297 us; the launch traced here: 294 us
  Pallas kernels  261 us (88%)
  matrix products  19 us (6%)
  local copies, waits for them, and re-layouts  14.3 us (5%)
    pallas_call x1, Pallas kernels, doubles(): pl.pallas_call(functools.partial(whole_kernel, nb, nc, chunks), out_shape...  261 us
    dot_general x1, matrix products, on_device(): jnp.einsum('mad,mxd->ax', r_pairs[0], flat, preferred_element_type=F32)  19 us
    unnamed x6, local copies, waits for them, and re-layouts  12.3 us

commit v1 on v0

--- a/solution.py
+++ b/solution.py
@@ -10,15 +10,16 @@
 MESH = pl.DeviceIdType.MESH
 CHUNKS = 8
 GROUP = 16
-SLOTS = 4
-LANES = 128
+HALF = 8
+TURNS = 3
+FIRST = 64
 BF16, F32 = jnp.bfloat16, jnp.float32
 
 
 def whole_kernel(nb, nc, chunks, *refs):
-    cube, w_tiles, base_a, energy_b, energy_c, sigma = refs[:6]
-    slab, turned, summed, home, combined, w_slots, total = refs[6:13]
-    halved, dealt, spread_out = refs[13:-8], refs[-8], refs[-7]
+    r_rows, w_tiles, base_a, energy_b, energy_c, sigma = refs[:6]
+    slab, turned, summed, home, pool, w_slots, raw, total = refs[6:14]
+    halved, dealt, spread_out = refs[14:-8], refs[-8], refs[-7]
     out_sems, in_sems, own_sems, w_sems, send_sems, got_sems = refs[-6:]
     rows, bw, cw = slab.shape[2:]
     width = nb * bw
@@ -30,13 +31,12 @@
         pl.semaphore_signal(barrier, inc=1, device_id=(b_me ^ step, c_me), device_id_type=MESH)
     for step in range(1, nc):
         pl.semaphore_signal(barrier, inc=1, device_id=(b_me, c_me ^ step), device_id_type=MESH)
-    pl.semaphore_wait(barrier, nb + nc - 2)
-
-    def spread(chunk):
+
+    def spread(chunk, part):
         for step in range(1, nb):
             pltpu.make_async_remote_copy(
-                src_ref=cube.at[b_me ^ step, chunk],
-                dst_ref=slab.at[chunk, b_me],
+                src_ref=pool.at[pl.ds((chunk * nb + (b_me ^ step)) * rows, rows), part],
+                dst_ref=slab.at[chunk, b_me, :, part],
                 send_sem=out_sems.at[0, chunk],
                 recv_sem=in_sems.at[0, chunk],
                 device_id=(b_me ^ step, c_me),
@@ -44,7 +44,9 @@
             ).start()
 
     def own_slab(chunk):
-        return pltpu.make_async_copy(cube.at[b_me, chunk], slab.at[chunk, b_me], own_sems.at[0, chunk])
+        return pltpu.make_async_copy(
+            pool.at[pl.ds((chunk * nb + b_me) * rows, rows)], slab.at[chunk, b_me], own_sems.at[0, chunk]
+        )
 
     def own_turned(chunk):
         return pltpu.make_async_copy(
@@ -102,7 +104,6 @@
     per = GROUP // rows
     steps = bw // GROUP
     row_c = energy_c[...]
-    pack = max(1, LANES // cw)
 
     def gathered(ref, index, block, inner):
         return jnp.concatenate([ref[index * per + n, block, :, inner, :] for n in range(per)], 0)
@@ -113,13 +114,11 @@
         mine = gathered(summed, b_step, block, a_inner).astype(F32)
         theirs = gathered(home, a_step, block, b_inner).astype(F32)
         both = mine + jnp.swapaxes(theirs, 0, 1)
-        a_rows = pl.ds(pl.multiple_of(block * bw + a_step * GROUP, GROUP), GROUP)
-        base = base_a[a_rows, :]
-        for b in range(0, GROUP, pack):
+        base = base_a[pl.ds(pl.multiple_of(block * bw + a_step * GROUP, GROUP), GROUP), :]
+        for b in range(GROUP):
             place = b_step * GROUP + b
-            entries = [both[b + n] / (base - energy_b[place + n] - row_c) for n in range(pack)]
-            lanes = pl.ds(pl.multiple_of(place * cw, pack * cw), pack * cw)
-            combined[a_rows, lanes] = jnp.concatenate(entries, 1).astype(BF16)
+            below = base - energy_b[place] - row_c
+            pool[place * nb + block, a_inner, :] = (both[b] / below).astype(BF16)
 
     def widen(step):
         for n in range(per):
@@ -136,46 +135,48 @@
     part_width = width // 2
     units = 6
     tiles = bw // GROUP
-    depth = GROUP * cw
 
     def fetch(index):
         unit, tile = index // tiles, index % tiles
-        slot = index % SLOTS
-        return pltpu.make_async_copy(
-            w_tiles.at[
-                0,
-                unit // 2,
-                pl.ds(tile * GROUP, GROUP),
-                :,
-                pl.ds(pl.multiple_of((unit % 2) * part_width, part_width), part_width),
-            ],
-            w_slots.at[slot],
-            w_sems.at[slot],
-        )
+        lanes = pl.ds(pl.multiple_of((unit % 2) * part_width, part_width), part_width)
+        copies = []
+        for side in range(2):
+            slot = (index % TURNS) * 2 + side
+            source = w_tiles.at[0, unit // 2, pl.ds(tile * GROUP + side * HALF, HALF), :, lanes]
+            target = w_slots.at[slot, :, :, pl.ds(0, part_width)]
+            copies.append(pltpu.make_async_copy(source, target, w_sems.at[slot]))
+        return copies
 
     def product(unit):
-        where = [unit // 2] + [slice(None)] * bits + [slice(None), pl.ds((unit % 2) * part_width, part_width)]
+        where = tuple([unit // 2] + [slice(None)] * bits + [slice(None), pl.ds((unit % 2) * part_width, part_width)])
 
         @pl.loop(0, tiles)
         def _(tile):
             index = unit * tiles + tile
-            fetch(index).wait()
-            entries = combined[:, pl.ds(pl.multiple_of(tile * depth, depth), depth)]
-            piece = jnp.dot(
-                entries, w_slots[index % SLOTS].reshape(depth, part_width), preferred_element_type=F32
-            ).reshape([2] * bits + [bw, part_width])
+            for copy in fetch(index):
+                copy.wait()
+            first = tile * GROUP
+            entries = jnp.concatenate(
+                [pool[pl.ds((first + n) * nb, nb)].reshape(width, cw) for n in range(GROUP)], 1
+            )
+            slot = (index % TURNS) * 2
+            factors = jnp.concatenate(
+                [w_slots[slot + side, :, :, :part_width].reshape(HALF * cw, part_width) for side in range(2)], 0
+            )
+            piece = jnp.dot(entries, factors, preferred_element_type=F32).reshape([2] * bits + [bw, part_width])
 
             @pl.when(tile == 0)
             def _():
-                total[tuple(where)] = piece
+                total[where] = piece
 
             @pl.when(tile > 0)
             def _():
-                total[tuple(where)] = total[tuple(where)] + piece
-
-            @pl.when(index + SLOTS < units * tiles)
+                total[where] = total[where] + piece
+
+            @pl.when(index + TURNS < units * tiles)
             def _():
-                fetch(index + SLOTS).start()
+                for copy in fetch(index + TURNS):
+                    copy.start()
 
     def bit(place):
         return (b_me // (1 << place)) % 2
@@ -245,13 +246,93 @@
                 result = result + spread_out[unit // 2, c_me ^ step]
             sigma[unit // 2] = result
 
-    for index in range(SLOTS):
-        fetch(index).start()
-
-    @pl.loop(0, chunks)
+    def pass_on(chunk):
+        arrived(0, chunk)
+        own_slab(chunk).wait()
+        turn(chunk)
+        own_turned(chunk).start()
+
+    ahead = FIRST // (nb * rows)
+    passes = ((0, ahead), (ahead, chunks - ahead))
+
+    def cube_fetch(group, side, pair):
+        slot = side * 3 + pair
+        source = w_tiles.at[0, pair, pl.ds(group * GROUP + side * HALF, HALF)]
+        return pltpu.make_async_copy(source, w_slots.at[slot], w_sems.at[slot])
+
+    def cube_pass(number):
+        start, count = passes[number]
+        base, height = start * nb * rows, count * nb * rows
+        last = number == len(passes) - 1
+
+        @pl.loop(0, tiles)
+        def _(group):
+            for side in range(2):
+                for pair in range(3):
+                    cube_fetch(group, side, pair).wait()
+                for n in range(0, HALF, 2):
+                    value = None
+                    for pair in range(3):
+                        factors = w_slots[side * 3 + pair, n : n + 2].reshape(2 * cw, width)
+                        term = lax.dot_general(
+                            r_rows[pair, base : base + height],
+                            factors,
+                            (((1,), (1,)), ((), ())),
+                            preferred_element_type=F32,
+                        )
+                        value = term if value is None else value + term
+                    at = (side * HALF + n) * cw
+                    raw[:height, at : at + 2 * cw] = value
+                for pair in range(3):
+                    if last:
+                        pl.when(group + 1 < tiles)(cube_fetch(group + 1, side, pair).start)
+                    else:
+                        cube_fetch((group + 1) % tiles, side, pair).start()
+            inner = pl.ds(pl.multiple_of(group * GROUP, GROUP), GROUP)
+
+            @pl.loop(0, height // GROUP)
+            def _(place):
+                entries = raw[pl.ds(pl.multiple_of(place * GROUP, GROUP), GROUP), :]
+                split = jnp.stack([entries[:, n * cw : (n + 1) * cw] for n in range(GROUP)], 0)
+                pool[pl.ds(base + place * GROUP, GROUP), inner, :] = jnp.swapaxes(split, 0, 1).astype(BF16)
+
+            if number == 0:
+
+                @pl.when(group == 0)
+                def _():
+                    pl.semaphore_wait(barrier, nb + nc - 2)
+
+                for chunk in range(start, start + count):
+                    spread(chunk, inner)
+            else:
+
+                @pl.when(group == 0)
+                def _():
+                    for chunk in range(start):
+                        pass_on(chunk)
+
+        if number > 0:
+
+            @pl.loop(start, start + count)
+            def _(chunk):
+                spread(chunk, pl.ds(0, bw))
+
+        @pl.loop(start, start + count)
+        def _(chunk):
+            own_slab(chunk).start()
+
+    for side in range(2):
+        for pair in range(3):
+            cube_fetch(0, side, pair).start()
+    for number in range(len(passes)):
+        cube_pass(number)
+    for index in range(TURNS):
+        for copy in fetch(index):
+            copy.start()
+
+    @pl.loop(ahead, chunks)
     def _(chunk):
-        spread(chunk)
-        own_slab(chunk).start()
+        own_slab(chunk).wait()
 
     def settle(chunk):
         arrived(1, chunk)
@@ -261,15 +342,18 @@
         own_home(chunk).start()
 
     for chunk in range(chunks):
-        arrived(0, chunk)
-        own_slab(chunk).wait()
-        turn(chunk)
-        own_turned(chunk).start()
+        if chunk >= ahead:
+            arrived(0, chunk)
+            turn(chunk)
+            own_turned(chunk).start()
         if chunk > 0:
             settle(chunk - 1)
-        early = steps - chunks + chunk - 1
-        if early >= 0:
-            widen(early)
+        for step in range(steps - 1):
+            if chunk == chunks - 1 - max(1, per // 2) * (steps - 2 - step):
+                if step == 0:
+                    for number in range(chunks):
+                        left(0, number)
+                widen(step)
     settle(chunks - 1)
     widen(steps - 1)
 
@@ -295,13 +379,13 @@
 
     @pl.loop(0, chunks)
     def _(chunk):
-        for kind in range(3):
+        for kind in range(1, 3):
             left(kind, chunk)
 
 
-def doubles(cubes, w_tiles, base_a, energy_b, energy_c, nb, nc):
-    chunks, rows, bw, cw = cubes.shape[1:]
-    width = nb * bw
+def doubles(r_rows, w_tiles, base_a, energy_b, energy_c, nb, nc):
+    bw, cw, width = w_tiles.shape[2:]
+    chunks, rows = CHUNKS, bw // CHUNKS
     bits = nb.bit_length() - 1
     block = (rows, bw, cw)
     vmem = pl.BlockSpec(memory_space=pltpu.VMEM)
@@ -309,15 +393,16 @@
     return pl.pallas_call(
         functools.partial(whole_kernel, nb, nc, chunks),
         out_shape=jax.ShapeDtypeStruct((3, bw, cw), F32),
-        in_specs=[hbm, hbm, vmem, pl.BlockSpec(memory_space=pltpu.SMEM), vmem],
+        in_specs=[vmem, hbm, vmem, pl.BlockSpec(memory_space=pltpu.SMEM), vmem],
         out_specs=vmem,
         scratch_shapes=[
             pltpu.VMEM((chunks, nb) + block, BF16),
             pltpu.VMEM((chunks, nc, nb // nc) + block, BF16),
             pltpu.VMEM((chunks, nb) + block, BF16),
             pltpu.VMEM((chunks, nb) + block, BF16),
-            pltpu.VMEM((width, bw * cw), BF16),
-            pltpu.VMEM((SLOTS, GROUP, cw, width // 2), BF16),
+            pltpu.VMEM((width, bw, cw), BF16),
+            pltpu.VMEM((6, HALF, cw, width), BF16),
+            pltpu.VMEM((width - FIRST, GROUP * cw), F32),
             pltpu.VMEM((3,) + (2,) * bits + (bw, width), F32),
         ]
         + [pltpu.VMEM((6,) + (2,) * (bits - 1 - stage) + (bw, width // 2), F32) for stage in range(bits)]
@@ -327,14 +412,14 @@
             pltpu.SemaphoreType.DMA((3, chunks)),
             pltpu.SemaphoreType.DMA((3, chunks)),
             pltpu.SemaphoreType.DMA((3, chunks)),
-            pltpu.SemaphoreType.DMA((SLOTS,)),
+            pltpu.SemaphoreType.DMA((6,)),
             pltpu.SemaphoreType.DMA((6, bits + nc // 2)),
             pltpu.SemaphoreType.DMA((6, bits + 1)),
         ],
         compiler_params=pltpu.CompilerParams(
             collective_id=0, has_side_effects=True, vmem_limit_bytes=60 << 20
         ),
-    )(cubes, w_tiles, base_a, energy_b, energy_c)
+    )(r_rows, w_tiles, base_a, energy_b, energy_c)
 
 
 def on_device(r_pairs, w_tiles, virt_energy, energy_shift):
@@ -344,10 +429,8 @@
     energy_b = lax.dynamic_slice_in_dim(virt_energy, lax.axis_index("ba") * bw, bw)
     energy_c = lax.dynamic_slice_in_dim(virt_energy, lax.axis_index("col") * cw, cw)
     base_a = jnp.broadcast_to((energy_shift - virt_energy)[:, None], (width, cw))
-    flat = w_tiles.reshape(3, bw * cw, width)
-    cubes = jnp.einsum("mad,mxd->ax", r_pairs[0], flat, preferred_element_type=F32)
-    cubes = cubes.astype(BF16).reshape(nb, CHUNKS, bw // CHUNKS, bw, cw)
-    return doubles(cubes, w_tiles, base_a, energy_b, energy_c[None], nb, nc)[None]
+    r_rows = r_pairs[0].reshape(3, nb, CHUNKS, bw // CHUNKS, width).swapaxes(1, 2).reshape(3, width, width)
+    return doubles(r_rows, w_tiles, base_a, energy_b, energy_c[None], nb, nc)[None]
 
 
 def solution(mesh):

time: 297 us -> 277 us (0.933)
  matrix products: 19 us -> 0 us
  local copies, waits for them, and re-layouts: 14.3 us -> 7.75 us
  Pallas kernels: 261 us -> 266 us
    dot_general x1 -> x0, matrix products: 19 us -> none  [on_device(): jnp.einsum('mad,mxd->ax', r_pairs[0], flat, preferred_element_type=F32)]
    unnamed x6 -> x1, local copies, waits for them, and re-layouts: 12.3 us -> 1.54 us
    pallas_call x1, Pallas kernels: 261 us -> 266 us  [doubles(): pl.pallas_call(functools.partial(whole_kernel, nb, nc, chunks), out_shape...]
where the time goes in v1:
time: 277 us; the launch traced here: 275 us
  Pallas kernels  266 us (96%)
  local copies, waits for them, and re-layouts  7.75 us (3%)
    pallas_call x1, Pallas kernels, doubles(): pl.pallas_call(functools.partial(whole_kernel, nb, nc, chunks), out_shape...  266 us

profile of v1, /device:TPU:0, one launch (start us, length us, event | category | flops | bytes accessed | tf_op | source)
XLA Modules:
  0.0 275.2 jit_solution(3884626045748019792)
XLA Ops:
  0.7 1.3 dynamic-slice_bitcast_fusion.refs_4_
  2.0 1.3 dynamic_slice.6.refs_3_
  3.3 0.7 broadcast_subtract_fusion
  3.9 0.8 broadcast_in_dim.12.refs_2_
  4.8 2.8 %copy.5 = bf16[3,8,8,8,512]{4,3,1,2,0:T(8,128)(2,1)} copy(bf16[3,8,8,8,512]{4,3,2,1,0:T(8,128)(2,1)} %bitcast.10) | data formatting | bytes 3145728 | tf_op jit(solution)/shard_map/reshape;squeeze | solution.py:432
  7.6 266.1 %shard_map.46 = f32[3,64,128]{2,1,0:T(8,128)} custom-call(bf16[3,512,512]{2,1,0:T(8,128)(2,1)} %bitcast.9, bf16[1,3,64,128,512]{4,3,2,1,0:T(8,128)(2,1)} %refs_1_.1, f32[512,128]{1,0:T(8,128)} %broadcast_in_dim.12.refs_2_, f32[64]{0:T(128)} %dynamic_slice.6.refs_3_, f32[1,128]{1,0:T(1,128)} %dynamic-slice_bitcast_fusion.refs_4_), custom_call_target="tpu_custom_call" | custom-call | tf_op jit(solution)/shard_map/pallas_call | solution.py:393
  273.7 1.5 copy.8

commit v2 on v1

--- a/solution.py
+++ b/solution.py
@@ -8,23 +8,22 @@
 from jax.sharding import PartitionSpec as P
 
 MESH = pl.DeviceIdType.MESH
-CHUNKS = 8
+CHUNKS = 16
 GROUP = 16
 HALF = 8
 TURNS = 3
-FIRST = 64
 BF16, F32 = jnp.bfloat16, jnp.float32
 
 
 def whole_kernel(nb, nc, chunks, *refs):
-    r_rows, w_tiles, base_a, energy_b, energy_c, sigma = refs[:6]
-    slab, turned, summed, home, pool, w_slots, raw, total = refs[6:14]
-    halved, dealt, spread_out = refs[14:-8], refs[-8], refs[-7]
-    out_sems, in_sems, own_sems, w_sems, send_sems, got_sems = refs[-6:]
+    r_pairs, w_tiles, energy, energy_rows, shift, sigma = refs[:6]
+    slab, turned, summed, home, pool, r_rows, base_a, w_slots, raw, total = refs[6:16]
+    paired, gathered_in, dealt, spread_out = refs[16:20]
+    out_sems, in_sems, own_sems, w_sems, r_sems, send_sems, got_sems = refs[20:]
     rows, bw, cw = slab.shape[2:]
     width = nb * bw
     ratio = nb // nc
-    bits = nb.bit_length() - 1
+    chips, per, steps = nb // 2, GROUP // rows, bw // GROUP
     b_me, c_me = lax.axis_index("ba"), lax.axis_index("col")
     barrier = pltpu.get_barrier_semaphore()
     for step in range(1, nb):
@@ -32,10 +31,13 @@
     for step in range(1, nc):
         pl.semaphore_signal(barrier, inc=1, device_id=(b_me, c_me ^ step), device_id_type=MESH)
 
+    def block_rows(chunk, block):
+        return pl.ds((chunk // per * nb + block) * GROUP + chunk % per * rows, rows)
+
     def spread(chunk, part):
         for step in range(1, nb):
             pltpu.make_async_remote_copy(
-                src_ref=pool.at[pl.ds((chunk * nb + (b_me ^ step)) * rows, rows), part],
+                src_ref=pool.at[block_rows(chunk, b_me ^ step), part],
                 dst_ref=slab.at[chunk, b_me, :, part],
                 send_sem=out_sems.at[0, chunk],
                 recv_sem=in_sems.at[0, chunk],
@@ -45,7 +47,7 @@
 
     def own_slab(chunk):
         return pltpu.make_async_copy(
-            pool.at[pl.ds((chunk * nb + b_me) * rows, rows)], slab.at[chunk, b_me], own_sems.at[0, chunk]
+            pool.at[block_rows(chunk, b_me)], slab.at[chunk, b_me], own_sems.at[0, chunk]
         )
 
     def own_turned(chunk):
@@ -101,9 +103,7 @@
                     kept = slab[chunk, block, row].astype(F32)
                     summed[chunk, block, row] = (kept + flipped[part * bw : (part + 1) * bw]).astype(BF16)
 
-    per = GROUP // rows
-    steps = bw // GROUP
-    row_c = energy_c[...]
+    row_c = energy_rows[pl.ds(c_me, 1), :]
 
     def gathered(ref, index, block, inner):
         return jnp.concatenate([ref[index * per + n, block, :, inner, :] for n in range(per)], 0)
@@ -117,7 +117,7 @@
         base = base_a[pl.ds(pl.multiple_of(block * bw + a_step * GROUP, GROUP), GROUP), :]
         for b in range(GROUP):
             place = b_step * GROUP + b
-            below = base - energy_b[place] - row_c
+            below = base - energy[b_me * bw + place] - row_c
             pool[place * nb + block, a_inner, :] = (both[b] / below).astype(BF16)
 
     def widen(step):
@@ -147,8 +147,11 @@
             copies.append(pltpu.make_async_copy(source, target, w_sems.at[slot]))
         return copies
 
+    def lanes_of(unit):
+        return pl.ds((unit % 2) * part_width, part_width)
+
     def product(unit):
-        where = tuple([unit // 2] + [slice(None)] * bits + [slice(None), pl.ds((unit % 2) * part_width, part_width)])
+        where = (unit // 2, slice(None), slice(None), slice(None), lanes_of(unit))
 
         @pl.loop(0, tiles)
         def _(tile):
@@ -163,7 +166,7 @@
             factors = jnp.concatenate(
                 [w_slots[slot + side, :, :, :part_width].reshape(HALF * cw, part_width) for side in range(2)], 0
             )
-            piece = jnp.dot(entries, factors, preferred_element_type=F32).reshape([2] * bits + [bw, part_width])
+            piece = jnp.dot(entries, factors, preferred_element_type=F32).reshape(chips, 2, bw, part_width)
 
             @pl.when(tile == 0)
             def _():
@@ -178,35 +181,37 @@
                 for copy in fetch(index + TURNS):
                     copy.start()
 
-    def bit(place):
-        return (b_me // (1 << place)) % 2
-
-    def order(unit):
-        return list(range(bits)) if unit % 2 == 0 else [0] + list(range(1, bits))[::-1]
-
-    def region(unit, fixed):
-        lanes = pl.ds((unit % 2) * part_width, part_width)
-        picks = [fixed.get(place, slice(None)) for place in range(bits)[::-1]]
-        return tuple([unit // 2] + picks + [slice(None), lanes])
-
-    def halving(unit, stage):
-        done = order(unit)[:stage]
-        place = order(unit)[stage]
-        fixed = {n: bit(n) for n in done}
-        fixed[place] = 1 - bit(place)
+    core, chip = b_me % 2, b_me // 2
+
+    def pair_up(unit):
         return pltpu.make_async_remote_copy(
-            src_ref=total.at[region(unit, fixed)],
-            dst_ref=halved[stage].at[unit],
-            send_sem=send_sems.at[unit, stage],
-            recv_sem=got_sems.at[unit, stage],
-            device_id=(b_me ^ (1 << place), c_me),
+            src_ref=total.at[unit // 2, :, 1 - core, :, lanes_of(unit)],
+            dst_ref=paired.at[unit],
+            send_sem=send_sems.at[unit, 0],
+            recv_sem=got_sems.at[unit, 0],
+            device_id=(b_me ^ 1, c_me),
             device_id_type=MESH,
         )
 
-    def halved_add(unit, stage):
-        halving(unit, stage).wait_recv()
-        where = region(unit, {n: bit(n) for n in order(unit)[: stage + 1]})
-        total[where] = total[where] + halved[stage][unit]
+    def pair_add(unit):
+        pair_up(unit).wait_recv()
+        where = (unit // 2, slice(None), core, slice(None), lanes_of(unit))
+        total[where] = total[where] + paired[unit]
+
+    def gather_in(unit):
+        for step in range(1, chips):
+            pltpu.make_async_remote_copy(
+                src_ref=total.at[unit // 2, chip ^ step, core, :, lanes_of(unit)],
+                dst_ref=gathered_in.at[unit, chip],
+                send_sem=send_sems.at[unit, 1],
+                recv_sem=got_sems.at[unit, 1],
+                device_id=(b_me ^ (2 * step), c_me),
+                device_id_type=MESH,
+            ).start()
+
+    def wait_blocks(unit, sem):
+        blocks = gathered_in.at[unit, pl.ds(0, chips - 1)]
+        pltpu.make_async_copy(blocks, blocks, sem).wait()
 
     levels = nc // 2
 
@@ -215,14 +220,17 @@
         return level, pltpu.make_async_remote_copy(
             src_ref=dealt.at[unit, n],
             dst_ref=spread_out.at[unit // 2, c_me],
-            send_sem=send_sems.at[unit, bits + n],
-            recv_sem=got_sems.at[unit // 2, bits],
+            send_sem=send_sems.at[unit, 2 + n],
+            recv_sem=got_sems.at[unit // 2, 2],
             device_id=(b_me, level),
             device_id_type=MESH,
         )
 
     def deal_blocks(unit):
-        block = total[region(unit, {place: bit(place) for place in range(bits)})]
+        wait_blocks(unit, got_sems.at[unit, 1])
+        block = total[unit // 2, chip, core, :, lanes_of(unit)]
+        for step in range(1, chips):
+            block = block + gathered_in[unit, chip ^ step]
         for n in range(levels):
             dealt[unit, n] = block[:, n * cw : (n + 1) * cw]
 
@@ -240,7 +248,7 @@
         @pl.when(c_me // levels == unit % 2)
         def _():
             landed = spread_out.at[unit // 2, pl.ds(0, nc - 1)]
-            pltpu.make_async_copy(landed, landed, got_sems.at[unit // 2, bits]).wait()
+            pltpu.make_async_copy(landed, landed, got_sems.at[unit // 2, 2]).wait()
             result = dealt[unit, c_me % levels]
             for step in range(1, nc):
                 result = result + spread_out[unit // 2, c_me ^ step]
@@ -252,8 +260,8 @@
         turn(chunk)
         own_turned(chunk).start()
 
-    ahead = FIRST // (nb * rows)
-    passes = ((0, ahead), (ahead, chunks - ahead))
+    passes = ((0, 1), (1, steps))
+    early = min(2, per)
 
     def cube_fetch(group, side, pair):
         slot = side * 3 + pair
@@ -261,8 +269,8 @@
         return pltpu.make_async_copy(source, w_slots.at[slot], w_sems.at[slot])
 
     def cube_pass(number):
-        start, count = passes[number]
-        base, height = start * nb * rows, count * nb * rows
+        first, stop = passes[number]
+        base, height = first * nb * GROUP, (stop - first) * nb * GROUP
         last = number == len(passes) - 1
 
         @pl.loop(0, tiles)
@@ -275,7 +283,7 @@
                     for pair in range(3):
                         factors = w_slots[side * 3 + pair, n : n + 2].reshape(2 * cw, width)
                         term = lax.dot_general(
-                            r_rows[pair, base : base + height],
+                            r_rows[pair, first:stop].reshape(height, width),
                             factors,
                             (((1,), (1,)), ((), ())),
                             preferred_element_type=F32,
@@ -302,35 +310,44 @@
                 def _():
                     pl.semaphore_wait(barrier, nb + nc - 2)
 
-                for chunk in range(start, start + count):
-                    spread(chunk, inner)
+                spread(0, inner)
             else:
-
-                @pl.when(group == 0)
-                def _():
-                    for chunk in range(start):
+                for chunk in range(early):
+
+                    @pl.when(group == chunk * tiles // early)
+                    def _():
                         pass_on(chunk)
 
-        if number > 0:
-
-            @pl.loop(start, start + count)
-            def _(chunk):
-                spread(chunk, pl.ds(0, bw))
-
-        @pl.loop(start, start + count)
+        @pl.loop(max(first * per, 1), stop * per)
+        def _(chunk):
+            spread(chunk, pl.ds(0, bw))
+
+        @pl.loop(first * per, stop * per)
         def _(chunk):
             own_slab(chunk).start()
 
-    for side in range(2):
+    def r_fetch(pair, step):
+        return pltpu.make_async_copy(r_pairs.at[pair, :, step], r_rows.at[pair, step], r_sems.at[pair, step])
+
+    for step in range(steps):
         for pair in range(3):
-            cube_fetch(0, side, pair).start()
+            r_fetch(pair, step).start()
+            if step == 0:
+                for side in range(2):
+                    cube_fetch(0, side, pair).start()
+    for level in range(nc):
+        row = jnp.broadcast_to(energy_rows[level : level + 1, :], (cw, cw))
+        base_a[level * cw : (level + 1) * cw, :] = shift[0] - row.T
     for number in range(len(passes)):
+        for step in range(*passes[number]):
+            for pair in range(3):
+                r_fetch(pair, step).wait()
         cube_pass(number)
     for index in range(TURNS):
         for copy in fetch(index):
             copy.start()
 
-    @pl.loop(ahead, chunks)
+    @pl.loop(early, chunks)
     def _(chunk):
         own_slab(chunk).wait()
 
@@ -342,7 +359,7 @@
         own_home(chunk).start()
 
     for chunk in range(chunks):
-        if chunk >= ahead:
+        if chunk >= early:
             arrived(0, chunk)
             turn(chunk)
             own_turned(chunk).start()
@@ -357,24 +374,24 @@
     settle(chunks - 1)
     widen(steps - 1)
 
-    for time in range(units + bits + 1):
+    for time in range(units + 3):
         if time < units:
             product(time)
-        for stage in range(bits):
-            if 0 <= time - stage - 1 < units:
-                halved_add(time - stage - 1, stage)
-        if 0 <= time - bits < units:
-            deal_blocks(time - bits)
-        for stage in range(bits):
-            if 0 <= time - stage < units:
-                halving(time - stage, stage).start()
-        if 0 <= time - bits < units:
-            deal_start(time - bits)
-        if 0 <= time - bits - 1 < units:
-            finish(time - bits - 1)
+        if 0 <= time - 1 < units:
+            pair_add(time - 1)
+        if 0 <= time - 2 < units:
+            deal_blocks(time - 2)
+        if time < units:
+            pair_up(time).start()
+        if 0 <= time - 1 < units:
+            gather_in(time - 1)
+        if 0 <= time - 2 < units:
+            deal_start(time - 2)
+        if 0 <= time - 3:
+            finish(time - 3)
     for unit in range(units):
-        for stage in range(bits):
-            halving(unit, stage).wait_send()
+        pair_up(unit).wait_send()
+        wait_blocks(unit, send_sems.at[unit, 1])
         deal_sent(unit)
 
     @pl.loop(0, chunks)
@@ -383,17 +400,17 @@
             left(kind, chunk)
 
 
-def doubles(r_rows, w_tiles, base_a, energy_b, energy_c, nb, nc):
+def doubles(r_pairs, w_tiles, energy, shift, nb, nc):
     bw, cw, width = w_tiles.shape[2:]
     chunks, rows = CHUNKS, bw // CHUNKS
-    bits = nb.bit_length() - 1
+    steps = bw // GROUP
     block = (rows, bw, cw)
-    vmem = pl.BlockSpec(memory_space=pltpu.VMEM)
+    vmem, smem = pl.BlockSpec(memory_space=pltpu.VMEM), pl.BlockSpec(memory_space=pltpu.SMEM)
     hbm = pl.BlockSpec(memory_space=pl.ANY)
     return pl.pallas_call(
         functools.partial(whole_kernel, nb, nc, chunks),
         out_shape=jax.ShapeDtypeStruct((3, bw, cw), F32),
-        in_specs=[vmem, hbm, vmem, pl.BlockSpec(memory_space=pltpu.SMEM), vmem],
+        in_specs=[hbm, hbm, smem, vmem, smem],
         out_specs=vmem,
         scratch_shapes=[
             pltpu.VMEM((chunks, nb) + block, BF16),
@@ -401,36 +418,32 @@
             pltpu.VMEM((chunks, nb) + block, BF16),
             pltpu.VMEM((chunks, nb) + block, BF16),
             pltpu.VMEM((width, bw, cw), BF16),
+            pltpu.VMEM((3, steps, nb, GROUP, width), BF16),
+            pltpu.VMEM((width, cw), F32),
             pltpu.VMEM((6, HALF, cw, width), BF16),
-            pltpu.VMEM((width - FIRST, GROUP * cw), F32),
-            pltpu.VMEM((3,) + (2,) * bits + (bw, width), F32),
-        ]
-        + [pltpu.VMEM((6,) + (2,) * (bits - 1 - stage) + (bw, width // 2), F32) for stage in range(bits)]
-        + [
+            pltpu.VMEM((width - nb * GROUP, GROUP * cw), F32),
+            pltpu.VMEM((3, nb // 2, 2, bw, width), F32),
+            pltpu.VMEM((6, nb // 2, bw, width // 2), F32),
+            pltpu.VMEM((6, nb // 2, bw, width // 2), F32),
             pltpu.VMEM((6, nc // 2, bw, cw), F32),
             pltpu.VMEM((3, nc, bw, cw), F32),
             pltpu.SemaphoreType.DMA((3, chunks)),
             pltpu.SemaphoreType.DMA((3, chunks)),
             pltpu.SemaphoreType.DMA((3, chunks)),
             pltpu.SemaphoreType.DMA((6,)),
-            pltpu.SemaphoreType.DMA((6, bits + nc // 2)),
-            pltpu.SemaphoreType.DMA((6, bits + 1)),
+            pltpu.SemaphoreType.DMA((3, steps)),
+            pltpu.SemaphoreType.DMA((6, 2 + nc // 2)),
+            pltpu.SemaphoreType.DMA((6, 3)),
         ],
         compiler_params=pltpu.CompilerParams(
             collective_id=0, has_side_effects=True, vmem_limit_bytes=60 << 20
         ),
-    )(r_rows, w_tiles, base_a, energy_b, energy_c)
+    )(r_pairs.reshape(3, nb, steps, GROUP, width), w_tiles, energy, energy.reshape(nc, cw), shift)
 
 
 def on_device(r_pairs, w_tiles, virt_energy, energy_shift):
-    width = w_tiles.shape[4]
-    bw, cw = w_tiles.shape[2], w_tiles.shape[3]
     nb, nc = lax.axis_size("ba"), lax.axis_size("col")
-    energy_b = lax.dynamic_slice_in_dim(virt_energy, lax.axis_index("ba") * bw, bw)
-    energy_c = lax.dynamic_slice_in_dim(virt_energy, lax.axis_index("col") * cw, cw)
-    base_a = jnp.broadcast_to((energy_shift - virt_energy)[:, None], (width, cw))
-    r_rows = r_pairs[0].reshape(3, nb, CHUNKS, bw // CHUNKS, width).swapaxes(1, 2).reshape(3, width, width)
-    return doubles(r_rows, w_tiles, base_a, energy_b, energy_c[None], nb, nc)[None]
+    return doubles(r_pairs, w_tiles, virt_energy, energy_shift, nb, nc)[None]
 
 
 def solution(mesh):

time: 277 us -> 258 us (0.931)
  Pallas kernels: 266 us -> 255 us
  local copies, waits for them, and re-layouts: 7.75 us -> 1.54 us
    pallas_call x1, Pallas kernels: 266 us -> 255 us  [doubles(): pl.pallas_call(functools.partial(whole_kernel, nb, nc, chunks), out_shape...]
where the time goes in v2:
time: 258 us; the launch traced here: 257 us
  Pallas kernels  255 us (99%)
    pallas_call x1, Pallas kernels, doubles(): pl.pallas_call(functools.partial(whole_kernel, nb, nc, chunks), out_shape...  255 us

profile of v2, /device:TPU:0, one launch (start us, length us, event | category | flops | bytes accessed | tf_op | source)
XLA Modules:
  0.0 256.7 jit_solution(16241064292059283786)
XLA Ops:
  0.7 254.5 %shard_map.46 = f32[3,64,128]{2,1,0:T(8,128)} custom-call(bf16[3,8,4,16,512]{4,3,2,1,0:T(8,128)(2,1)} %bitcast.3, bf16[1,3,64,128,512]{4,3,2,1,0:T(8,128)(2,1)} %refs_1_.1, f32[512]{0:T(512)} %refs_2_.1, f32[4,128]{1,0:T(4,128)} %bitcast.5, f32[1]{0:T(128)S(6)} %copy.6.refs_4_), custom_call_target="tpu_custom_call" | custom-call | tf_op jit(solution)/shard_map/pallas_call | solution.py:410
  255.2 1.5 copy.7

commit v3 on v2

--- a/solution.py
+++ b/solution.py
@@ -12,14 +12,15 @@
 GROUP = 16
 HALF = 8
 TURNS = 3
+AHEAD = 2
 BF16, F32 = jnp.bfloat16, jnp.float32
 
 
 def whole_kernel(nb, nc, chunks, *refs):
     r_pairs, w_tiles, energy, energy_rows, shift, sigma = refs[:6]
     slab, turned, summed, home, pool, r_rows, base_a, w_slots, raw, total = refs[6:16]
-    paired, gathered_in, dealt, spread_out = refs[16:20]
-    out_sems, in_sems, own_sems, w_sems, r_sems, send_sems, got_sems = refs[20:]
+    paired, gathered_in, late_in, dealt, spread_out = refs[16:21]
+    out_sems, in_sems, own_sems, w_sems, r_sems, send_sems, got_sems = refs[21:]
     rows, bw, cw = slab.shape[2:]
     width = nb * bw
     ratio = nb // nc
@@ -120,10 +121,13 @@
             below = base - energy[b_me * bw + place] - row_c
             pool[place * nb + block, a_inner, :] = (both[b] / below).astype(BF16)
 
-    def widen(step):
+    def came_home(step):
         for n in range(per):
             arrived(2, step * per + n)
             own_home(step * per + n).wait()
+
+    def widen(step):
+        came_home(step)
 
         @pl.loop(0, (2 * step + 1) * nb)
         def _(place):
@@ -132,127 +136,160 @@
             b_step = jnp.where(cell <= step, cell, step)
             combine(a_step, b_step, block)
 
+    def widen_last_b():
+        @pl.loop(0, (steps - 1) * nb)
+        def _(place):
+            combine(place // nb, steps - 1, place % nb)
+
+    def widen_last_a():
+        came_home(steps - 1)
+
+        @pl.loop(0, steps * nb)
+        def _(place):
+            combine(steps - 1, place // nb, place % nb)
+
     part_width = width // 2
     units = 6
-    tiles = bw // GROUP
+    tiles = steps
+    before = units * (steps - 1)
+    items = before + units + units * steps
+    levels = nc // 2
+    core, chip = b_me % 2, b_me // 2
+    parts = (pl.ds(0, bw - GROUP), pl.ds(bw - GROUP, GROUP))
+    heights = (bw - GROUP, GROUP)
+
+    def item(index):
+        late = index - before - units
+        unit = jnp.where(
+            index < before, index // (steps - 1), jnp.where(late < 0, index - before, late // steps)
+        )
+        tile = jnp.where(index < before, index % (steps - 1), jnp.where(late < 0, steps - 1, late % steps))
+        return unit, tile
+
+    def lanes_of(unit):
+        return pl.ds(pl.multiple_of((unit % 2) * part_width, part_width), part_width)
 
     def fetch(index):
-        unit, tile = index // tiles, index % tiles
-        lanes = pl.ds(pl.multiple_of((unit % 2) * part_width, part_width), part_width)
+        unit, tile = item(index)
         copies = []
         for side in range(2):
             slot = (index % TURNS) * 2 + side
-            source = w_tiles.at[0, unit // 2, pl.ds(tile * GROUP + side * HALF, HALF), :, lanes]
+            source = w_tiles.at[0, unit // 2, pl.ds(tile * GROUP + side * HALF, HALF), :, lanes_of(unit)]
             target = w_slots.at[slot, :, :, pl.ds(0, part_width)]
             copies.append(pltpu.make_async_copy(source, target, w_sems.at[slot]))
         return copies
 
-    def lanes_of(unit):
-        return pl.ds((unit % 2) * part_width, part_width)
-
-    def product(unit):
-        where = (unit // 2, slice(None), slice(None), slice(None), lanes_of(unit))
-
-        @pl.loop(0, tiles)
-        def _(tile):
-            index = unit * tiles + tile
-            for copy in fetch(index):
-                copy.wait()
-            first = tile * GROUP
-            entries = jnp.concatenate(
-                [pool[pl.ds((first + n) * nb, nb)].reshape(width, cw) for n in range(GROUP)], 1
-            )
-            slot = (index % TURNS) * 2
-            factors = jnp.concatenate(
-                [w_slots[slot + side, :, :, :part_width].reshape(HALF * cw, part_width) for side in range(2)], 0
-            )
-            piece = jnp.dot(entries, factors, preferred_element_type=F32).reshape(chips, 2, bw, part_width)
-
-            @pl.when(tile == 0)
-            def _():
-                total[where] = piece
-
-            @pl.when(tile > 0)
-            def _():
-                total[where] = total[where] + piece
-
-            @pl.when(index + TURNS < units * tiles)
-            def _():
-                for copy in fetch(index + TURNS):
-                    copy.start()
-
-    core, chip = b_me % 2, b_me // 2
+    def multiply(index, unit, tile, part):
+        for copy in fetch(index):
+            copy.wait()
+        first = tile * GROUP
+        entries = jnp.concatenate(
+            [pool[pl.ds((first + n) * nb, nb), parts[part]].reshape(nb * heights[part], cw) for n in range(GROUP)], 1
+        )
+        slot = (index % TURNS) * 2
+        factors = jnp.concatenate(
+            [w_slots[slot + side, :, :, :part_width].reshape(HALF * cw, part_width) for side in range(2)], 0
+        )
+        piece = jnp.dot(entries, factors, preferred_element_type=F32).reshape(chips, 2, heights[part], part_width)
+        where = (unit // 2, slice(None), slice(None), parts[part], lanes_of(unit))
+
+        @pl.when(tile == 0)
+        def _():
+            total[where] = piece
+
+        @pl.when(tile > 0)
+        def _():
+            total[where] = total[where] + piece
+
+        @pl.when(index + TURNS < items)
+        def _():
+            for copy in fetch(index + TURNS):
+                copy.start()
 
     def pair_up(unit):
         return pltpu.make_async_remote_copy(
-            src_ref=total.at[unit // 2, :, 1 - core, :, lanes_of(unit)],
-            dst_ref=paired.at[unit],
-            send_sem=send_sems.at[unit, 0],
-            recv_sem=got_sems.at[unit, 0],
+            src_ref=total.at[unit // 2, :, 1 - core, parts[0], lanes_of(unit)],
+            dst_ref=paired.at[unit, :, parts[0]],
+            send_sem=send_sems.at[0, unit, 0],
+            recv_sem=got_sems.at[0, unit, 0],
             device_id=(b_me ^ 1, c_me),
             device_id_type=MESH,
         )
 
     def pair_add(unit):
         pair_up(unit).wait_recv()
-        where = (unit // 2, slice(None), core, slice(None), lanes_of(unit))
-        total[where] = total[where] + paired[unit]
+        where = (unit // 2, slice(None), core, parts[0], lanes_of(unit))
+        total[where] = total[where] + paired[unit, :, parts[0]]
 
     def gather_in(unit):
         for step in range(1, chips):
             pltpu.make_async_remote_copy(
-                src_ref=total.at[unit // 2, chip ^ step, core, :, lanes_of(unit)],
-                dst_ref=gathered_in.at[unit, chip],
-                send_sem=send_sems.at[unit, 1],
-                recv_sem=got_sems.at[unit, 1],
+                src_ref=total.at[unit // 2, chip ^ step, core, parts[0], lanes_of(unit)],
+                dst_ref=gathered_in.at[unit, chip, parts[0]],
+                send_sem=send_sems.at[0, unit, 1],
+                recv_sem=got_sems.at[0, unit, 1],
                 device_id=(b_me ^ (2 * step), c_me),
                 device_id_type=MESH,
             ).start()
 
-    def wait_blocks(unit, sem):
-        blocks = gathered_in.at[unit, pl.ds(0, chips - 1)]
+    def wait_blocks(part, unit, sem):
+        blocks = (gathered_in.at[unit, pl.ds(0, chips - 1), parts[0]], late_in.at[unit, pl.ds(0, nb - 1)])[part]
         pltpu.make_async_copy(blocks, blocks, sem).wait()
 
-    levels = nc // 2
-
-    def deal(unit, n):
+    def scatter(unit):
+        for step in range(1, nb):
+            peer = b_me ^ step
+            pltpu.make_async_remote_copy(
+                src_ref=total.at[unit // 2, peer // 2, peer % 2, parts[1], lanes_of(unit)],
+                dst_ref=late_in.at[unit, b_me],
+                send_sem=send_sems.at[1, unit, 1],
+                recv_sem=got_sems.at[1, unit, 1],
+                device_id=(peer, c_me),
+                device_id_type=MESH,
+            ).start()
+
+    def deal(part, unit, n):
         level = (unit % 2) * levels + n
         return level, pltpu.make_async_remote_copy(
-            src_ref=dealt.at[unit, n],
-            dst_ref=spread_out.at[unit // 2, c_me],
-            send_sem=send_sems.at[unit, 2 + n],
-            recv_sem=got_sems.at[unit // 2, 2],
+            src_ref=dealt.at[unit, n, parts[part]],
+            dst_ref=spread_out.at[unit // 2, c_me, parts[part]],
+            send_sem=send_sems.at[part, unit, 2 + n],
+            recv_sem=got_sems.at[part, unit // 2, 2],
             device_id=(b_me, level),
             device_id_type=MESH,
         )
 
-    def deal_blocks(unit):
-        wait_blocks(unit, got_sems.at[unit, 1])
-        block = total[unit // 2, chip, core, :, lanes_of(unit)]
-        for step in range(1, chips):
-            block = block + gathered_in[unit, chip ^ step]
+    def deal_blocks(part, unit):
+        wait_blocks(part, unit, got_sems.at[part, unit, 1])
+        block = total[unit // 2, chip, core, parts[part], lanes_of(unit)]
+        if part == 0:
+            for step in range(1, chips):
+                block = block + gathered_in[unit, chip ^ step, parts[0]]
+        else:
+            for step in range(1, nb):
+                block = block + late_in[unit, b_me ^ step]
         for n in range(levels):
-            dealt[unit, n] = block[:, n * cw : (n + 1) * cw]
-
-    def deal_start(unit):
+            dealt[unit, n, parts[part]] = block[:, n * cw : (n + 1) * cw]
+
+    def deal_start(part, unit):
         for n in range(levels):
-            level, copy = deal(unit, n)
+            level, copy = deal(part, unit, n)
             pl.when(level != c_me)(copy.start)
 
-    def deal_sent(unit):
+    def deal_sent(part, unit):
         for n in range(levels):
-            level, copy = deal(unit, n)
+            level, copy = deal(part, unit, n)
             pl.when(level != c_me)(copy.wait_send)
 
-    def finish(unit):
+    def finish(part, unit):
         @pl.when(c_me // levels == unit % 2)
         def _():
-            landed = spread_out.at[unit // 2, pl.ds(0, nc - 1)]
-            pltpu.make_async_copy(landed, landed, got_sems.at[unit // 2, 2]).wait()
-            result = dealt[unit, c_me % levels]
+            landed = spread_out.at[unit // 2, pl.ds(0, nc - 1), parts[part]]
+            pltpu.make_async_copy(landed, landed, got_sems.at[part, unit // 2, 2]).wait()
+            result = dealt[unit, c_me % levels, parts[part]]
             for step in range(1, nc):
-                result = result + spread_out[unit // 2, c_me ^ step]
-            sigma[unit // 2] = result
+                result = result + spread_out[unit // 2, c_me ^ step, parts[part]]
+            sigma[unit // 2, parts[part]] = result
 
     def pass_on(chunk):
         arrived(0, chunk)
@@ -359,40 +396,68 @@
         own_home(chunk).start()
 
     for chunk in range(chunks):
-        if chunk >= early:
-            arrived(0, chunk)
-            turn(chunk)
-            own_turned(chunk).start()
+        for later in (range(early, AHEAD + 1) if chunk == 0 else (chunk + AHEAD,)):
+            if later < chunks:
+                arrived(0, later)
+                turn(later)
+                own_turned(later).start()
         if chunk > 0:
             settle(chunk - 1)
         for step in range(steps - 1):
-            if chunk == chunks - 1 - max(1, per // 2) * (steps - 2 - step):
+            if chunk == chunks - 2 - max(1, per // 2) * (steps - 2 - step):
                 if step == 0:
                     for number in range(chunks):
                         left(0, number)
                 widen(step)
+        if chunk >= chunks - 2:
+            half = before // 2
+            begin = half * (chunk - chunks + 2)
+
+            @pl.loop(begin, begin + half)
+            def _(index):
+                multiply(index, index // (steps - 1), index % (steps - 1), 0)
+
     settle(chunks - 1)
-    widen(steps - 1)
-
-    for time in range(units + 3):
+    widen_last_b()
+
+    @pl.loop(0, units)
+    def _(unit):
+        multiply(before + unit, unit, steps - 1, 0)
+        pair_up(unit).start()
+
+    @pl.loop(0, units)
+    def _(unit):
+        pair_add(unit)
+        gather_in(unit)
+
+    widen_last_a()
+
+    for time in range(units + 2):
         if time < units:
-            product(time)
-        if 0 <= time - 1 < units:
-            pair_add(time - 1)
+
+            @pl.loop(0, tiles)
+            def _(tile):
+                multiply(before + units + time * tiles + tile, time, tile, 1)
+
+        if time < units:
+            deal_blocks(0, time)
         if 0 <= time - 2 < units:
-            deal_blocks(time - 2)
+            deal_blocks(1, time - 2)
         if time < units:
-            pair_up(time).start()
-        if 0 <= time - 1 < units:
-            gather_in(time - 1)
+            scatter(time)
+            deal_start(0, time)
         if 0 <= time - 2 < units:
-            deal_start(time - 2)
-        if 0 <= time - 3:
-            finish(time - 3)
+            deal_start(1, time - 2)
     for unit in range(units):
+        for part in range(2):
+            finish(part, unit)
+
+    @pl.loop(0, units)
+    def _(unit):
         pair_up(unit).wait_send()
-        wait_blocks(unit, send_sems.at[unit, 1])
-        deal_sent(unit)
+        for part in range(2):
+            wait_blocks(part, unit, send_sems.at[part, unit, 1])
+            deal_sent(part, unit)
 
     @pl.loop(0, chunks)
     def _(chunk):
@@ -425,6 +490,7 @@
             pltpu.VMEM((3, nb // 2, 2, bw, width), F32),
             pltpu.VMEM((6, nb // 2, bw, width // 2), F32),
             pltpu.VMEM((6, nb // 2, bw, width // 2), F32),
+            pltpu.VMEM((6, nb, GROUP, width // 2), F32),
             pltpu.VMEM((6, nc // 2, bw, cw), F32),
             pltpu.VMEM((3, nc, bw, cw), F32),
             pltpu.SemaphoreType.DMA((3, chunks)),
@@ -432,8 +498,8 @@
             pltpu.SemaphoreType.DMA((3, chunks)),
             pltpu.SemaphoreType.DMA((6,)),
             pltpu.SemaphoreType.DMA((3, steps)),
-            pltpu.SemaphoreType.DMA((6, 2 + nc // 2)),
-            pltpu.SemaphoreType.DMA((6, 3)),
+            pltpu.SemaphoreType.DMA((2, 6, 2 + nc // 2)),
+            pltpu.SemaphoreType.DMA((2, 6, 3)),
         ],
         compiler_params=pltpu.CompilerParams(
             collective_id=0, has_side_effects=True, vmem_limit_bytes=60 << 20

time: 258 us -> 248 us (0.961)
  Pallas kernels: 255 us -> 245 us
    pallas_call x1, Pallas kernels: 255 us -> 245 us  [doubles(): pl.pallas_call(functools.partial(whole_kernel, nb, nc, chunks), out_shape...]
where the time goes in v3:
time: 248 us
  Pallas kernels  245 us (99%)
    pallas_call x1, Pallas kernels, doubles(): pl.pallas_call(functools.partial(whole_kernel, nb, nc, chunks), out_shape...  245 us

profile of v3, /device:TPU:0, one launch (start us, length us, event | category | flops | bytes accessed | tf_op | source)
XLA Modules:
  0.0 247.6 jit_solution(2751184427595558508)
XLA Ops:
  0.7 245.4 %shard_map.46 = f32[3,64,128]{2,1,0:T(8,128)} custom-call(bf16[3,8,4,16,512]{4,3,2,1,0:T(8,128)(2,1)} %bitcast.3, bf16[1,3,64,128,512]{4,3,2,1,0:T(8,128)(2,1)} %refs_1_.1, f32[512]{0:T(512)} %refs_2_.1, f32[4,128]{1,0:T(4,128)} %bitcast.5, f32[1]{0:T(128)S(6)} %copy.6.refs_4_), custom_call_target="tpu_custom_call" | custom-call | tf_op jit(solution)/shard_map/pallas_call | solution.py:475
  246.1 1.5 copy.7

commit v4 on v3

--- a/solution.py
+++ b/solution.py
@@ -13,6 +13,7 @@
 HALF = 8
 TURNS = 3
 AHEAD = 2
+LANES = 128
 BF16, F32 = jnp.bfloat16, jnp.float32
 
 
@@ -20,7 +21,7 @@
     r_pairs, w_tiles, energy, energy_rows, shift, sigma = refs[:6]
     slab, turned, summed, home, pool, r_rows, base_a, w_slots, raw, total = refs[6:16]
     paired, gathered_in, late_in, dealt, spread_out = refs[16:21]
-    out_sems, in_sems, own_sems, w_sems, r_sems, send_sems, got_sems = refs[21:]
+    out_sems, in_sems, own_sems, w_sems, held_sems, r_sems, send_sems, got_sems = refs[21:]
     rows, bw, cw = slab.shape[2:]
     width = nb * bw
     ratio = nb // nc
@@ -151,60 +152,158 @@
     part_width = width // 2
     units = 6
     tiles = steps
-    before = units * (steps - 1)
-    items = before + units + units * steps
     levels = nc // 2
     core, chip = b_me % 2, b_me // 2
     parts = (pl.ds(0, bw - GROUP), pl.ds(bw - GROUP, GROUP))
     heights = (bw - GROUP, GROUP)
 
-    def item(index):
-        late = index - before - units
-        unit = jnp.where(
-            index < before, index // (steps - 1), jnp.where(late < 0, index - before, late // steps)
-        )
-        tile = jnp.where(index < before, index % (steps - 1), jnp.where(late < 0, steps - 1, late % steps))
-        return unit, tile
-
     def lanes_of(unit):
         return pl.ds(pl.multiple_of((unit % 2) * part_width, part_width), part_width)
 
-    def fetch(index):
-        unit, tile = item(index)
+    def fetch(turn, unit, tile):
         copies = []
         for side in range(2):
-            slot = (index % TURNS) * 2 + side
+            slot = turn * 2 + side
             source = w_tiles.at[0, unit // 2, pl.ds(tile * GROUP + side * HALF, HALF), :, lanes_of(unit)]
             target = w_slots.at[slot, :, :, pl.ds(0, part_width)]
             copies.append(pltpu.make_async_copy(source, target, w_sems.at[slot]))
         return copies
 
-    def multiply(index, unit, tile, part):
-        for copy in fetch(index):
-            copy.wait()
-        first = tile * GROUP
+    def fetch_start(turn, unit, tile):
+        for copy in fetch(turn, unit, tile):
+            copy.start()
+
+    sides = cw // bw
+    fits = cw % LANES == 0 and per * sides == nb and sides == 2 and part_width == 2 * cw
+    held = chunks if fits else 0
+
+    def held_block(place, plane, block):
+        if plane == 0:
+            return slab.at[place, block]
+        return turned.at[place, block // ratio, block % ratio]
+
+    def hold(place):
+        unit, tile = place % units, place // units
+        for plane in range(2):
+            for block in range(nb):
+                source = w_tiles.at[
+                    0,
+                    unit // 2,
+                    pl.ds(tile * GROUP + block // sides * rows, rows),
+                    pl.ds(block % sides * bw, bw),
+                    pl.ds((unit % 2) * part_width + plane * cw, cw),
+                ]
+                target = held_block(place, plane, block)
+                pltpu.make_async_copy(source, target, held_sems.at[plane, place]).start()
+
+    def held_wait(place):
+        for plane, kept in enumerate((slab, turned)):
+            whole = kept.at[place]
+            pltpu.make_async_copy(whole, whole, held_sems.at[plane, place]).wait()
+
+    def held_factors(place):
+        planes = []
+        for plane in range(2):
+            blocks = [held_block(place, plane, block)[...] for block in range(nb)]
+            planes.append(
+                jnp.concatenate([blocks[n // rows * sides + side][n % rows] for n in range(GROUP) for side in range(sides)], 0)
+            )
+        return jnp.concatenate(planes, 1)
+
+    def slot_factors(turn):
+        return jnp.concatenate(
+            [w_slots[turn * 2 + side, :, :, :part_width].reshape(HALF * cw, part_width) for side in range(2)], 0
+        )
+
+    def multiply(factors, unit, tile, part):
         entries = jnp.concatenate(
-            [pool[pl.ds((first + n) * nb, nb), parts[part]].reshape(nb * heights[part], cw) for n in range(GROUP)], 1
-        )
-        slot = (index % TURNS) * 2
-        factors = jnp.concatenate(
-            [w_slots[slot + side, :, :, :part_width].reshape(HALF * cw, part_width) for side in range(2)], 0
+            [
+                pool[(tile * GROUP + n) * nb : (tile * GROUP + n + 1) * nb, parts[part]].reshape(
+                    nb * heights[part], cw
+                )
+                for n in range(GROUP)
+            ],
+            1,
         )
         piece = jnp.dot(entries, factors, preferred_element_type=F32).reshape(chips, 2, heights[part], part_width)
         where = (unit // 2, slice(None), slice(None), parts[part], lanes_of(unit))
-
-        @pl.when(tile == 0)
-        def _():
+        if tile == 0:
             total[where] = piece
-
-        @pl.when(tile > 0)
-        def _():
+        else:
             total[where] = total[where] + piece
 
-        @pl.when(index + TURNS < items)
-        def _():
-            for copy in fetch(index + TURNS):
-                copy.start()
+    def fetched(turn, unit, tile):
+        for copy in fetch(turn, unit, tile):
+            copy.wait()
+        return slot_factors(turn)
+
+    flowing = [tile for tile in range(steps - 1) if (tile + 1) * units > held]
+
+    def early_place(index, begin):
+        return begin + index // len(flowing), flowing[index % len(flowing)]
+
+    def early_start(begin):
+        for index in range(TURNS):
+            fetch_start(index, *early_place(index, begin))
+
+    def early_units(begin, stop):
+        if len(flowing) == 1:
+
+            @pl.loop(begin, stop)
+            def _(unit):
+                for tile in range(steps - 1):
+                    if tile in flowing:
+                        multiply(fetched(unit - begin, unit, tile), unit, tile, 0)
+
+                        @pl.when(unit + TURNS < units)
+                        def _():
+                            fetch_start(unit - begin, unit + TURNS, tile)
+                    else:
+                        held_wait(tile * units + unit)
+                        multiply(held_factors(tile * units + unit), unit, tile, 0)
+        else:
+            for index in range((stop - begin) * len(flowing)):
+                unit, tile = early_place(index, begin)
+                multiply(fetched(index % TURNS, unit, tile), unit, tile, 0)
+                later, place = early_place(index + TURNS, begin)
+                if later < units:
+                    fetch_start(index % TURNS, later, place)
+
+    def last_b_start():
+        for index in range(TURNS):
+            fetch_start(index, index, steps - 1)
+
+    def last_b_units():
+        @pl.loop(0, units // TURNS)
+        def _(lap):
+            for turn in range(TURNS):
+                unit = lap * TURNS + turn
+                multiply(fetched(turn, unit, steps - 1), unit, steps - 1, 0)
+
+                @pl.when(unit + TURNS < units)
+                def _():
+                    fetch_start(turn, unit + TURNS, steps - 1)
+
+                pair_up(unit).start()
+
+    stream = [(unit, tile) for unit in range(units) for tile in range(tiles) if tile * units + unit >= held]
+
+    def late_start():
+        for index in range(TURNS):
+            fetch_start(index, *stream[index])
+
+    def late_unit(unit):
+        for tile in range(tiles):
+            place = tile * units + unit
+            if place < held:
+                if tile in flowing or tile == steps - 1:
+                    held_wait(place)
+                multiply(held_factors(place), unit, tile, 1)
+            else:
+                index = stream.index((unit, tile))
+                multiply(fetched(index % TURNS, unit, tile), unit, tile, 1)
+                if index + TURNS < len(stream):
+                    fetch_start(index % TURNS, *stream[index + TURNS])
 
     def pair_up(unit):
         return pltpu.make_async_remote_copy(
@@ -232,19 +331,33 @@
                 device_id_type=MESH,
             ).start()
 
+    def late_pair(unit):
+        return pltpu.make_async_remote_copy(
+            src_ref=total.at[unit // 2, :, 1 - core, parts[1], lanes_of(unit)],
+            dst_ref=paired.at[unit, :, parts[1]],
+            send_sem=send_sems.at[1, unit, 0],
+            recv_sem=got_sems.at[1, unit, 0],
+            device_id=(b_me ^ 1, c_me),
+            device_id_type=MESH,
+        )
+
+    def late_add(unit):
+        late_pair(unit).wait_recv()
+        where = (unit // 2, slice(None), core, parts[1], lanes_of(unit))
+        total[where] = total[where] + paired[unit, :, parts[1]]
+
     def wait_blocks(part, unit, sem):
-        blocks = (gathered_in.at[unit, pl.ds(0, chips - 1), parts[0]], late_in.at[unit, pl.ds(0, nb - 1)])[part]
+        blocks = (gathered_in.at[unit, pl.ds(0, chips - 1), parts[0]], late_in.at[unit, pl.ds(0, chips - 1)])[part]
         pltpu.make_async_copy(blocks, blocks, sem).wait()
 
     def scatter(unit):
-        for step in range(1, nb):
-            peer = b_me ^ step
+        for step in range(1, chips):
             pltpu.make_async_remote_copy(
-                src_ref=total.at[unit // 2, peer // 2, peer % 2, parts[1], lanes_of(unit)],
-                dst_ref=late_in.at[unit, b_me],
+                src_ref=total.at[unit // 2, chip ^ step, core, parts[1], lanes_of(unit)],
+                dst_ref=late_in.at[unit, chip],
                 send_sem=send_sems.at[1, unit, 1],
                 recv_sem=got_sems.at[1, unit, 1],
-                device_id=(peer, c_me),
+                device_id=(b_me ^ (2 * step), c_me),
                 device_id_type=MESH,
             ).start()
 
@@ -266,8 +379,8 @@
             for step in range(1, chips):
                 block = block + gathered_in[unit, chip ^ step, parts[0]]
         else:
-            for step in range(1, nb):
-                block = block + late_in[unit, b_me ^ step]
+            for step in range(1, chips):
+                block = block + late_in[unit, chip ^ step]
         for n in range(levels):
             dealt[unit, n, parts[part]] = block[:, n * cw : (n + 1) * cw]
 
@@ -380,9 +493,7 @@
             for pair in range(3):
                 r_fetch(pair, step).wait()
         cube_pass(number)
-    for index in range(TURNS):
-        for copy in fetch(index):
-            copy.start()
+    early_start(0)
 
     @pl.loop(early, chunks)
     def _(chunk):
@@ -403,6 +514,10 @@
                 own_turned(later).start()
         if chunk > 0:
             settle(chunk - 1)
+        if chunk > 1:
+            left(1, chunk - 2)
+            if chunk - 2 < held:
+                hold(chunk - 2)
         for step in range(steps - 1):
             if chunk == chunks - 2 - max(1, per // 2) * (steps - 2 - step):
                 if step == 0:
@@ -410,20 +525,18 @@
                         left(0, number)
                 widen(step)
         if chunk >= chunks - 2:
-            half = before // 2
-            begin = half * (chunk - chunks + 2)
-
-            @pl.loop(begin, begin + half)
-            def _(index):
-                multiply(index, index // (steps - 1), index % (steps - 1), 0)
-
+            half = units // 2
+            early_units(half * (chunk - chunks + 2), half * (chunk - chunks + 3))
+    last_b_start()
     settle(chunks - 1)
+    for chunk in range(chunks - 2, chunks):
+        left(1, chunk)
+        if chunk < held:
+            hold(chunk)
     widen_last_b()
 
-    @pl.loop(0, units)
-    def _(unit):
-        multiply(before + unit, unit, steps - 1, 0)
-        pair_up(unit).start()
+    last_b_units()
+    late_start()
 
     @pl.loop(0, units)
     def _(unit):
@@ -432,22 +545,22 @@
 
     widen_last_a()
 
-    for time in range(units + 2):
-        if time < units:
-
-            @pl.loop(0, tiles)
-            def _(tile):
-                multiply(before + units + time * tiles + tile, time, tile, 1)
-
-        if time < units:
-            deal_blocks(0, time)
-        if 0 <= time - 2 < units:
-            deal_blocks(1, time - 2)
-        if time < units:
-            scatter(time)
-            deal_start(0, time)
-        if 0 <= time - 2 < units:
-            deal_start(1, time - 2)
+    for unit in range(units):
+        late_unit(unit)
+        if unit > 0:
+            late_add(unit - 1)
+            deal_blocks(0, unit - 1)
+        late_pair(unit).start()
+        if unit > 0:
+            scatter(unit - 1)
+            deal_start(0, unit - 1)
+    late_add(units - 1)
+    deal_blocks(0, units - 1)
+    scatter(units - 1)
+    deal_start(0, units - 1)
+    for unit in range(units):
+        deal_blocks(1, unit)
+        deal_start(1, unit)
     for unit in range(units):
         for part in range(2):
             finish(part, unit)
@@ -455,14 +568,14 @@
     @pl.loop(0, units)
     def _(unit):
         pair_up(unit).wait_send()
+        late_pair(unit).wait_send()
         for part in range(2):
             wait_blocks(part, unit, send_sems.at[part, unit, 1])
             deal_sent(part, unit)
 
     @pl.loop(0, chunks)
     def _(chunk):
-        for kind in range(1, 3):
-            left(kind, chunk)
+        left(2, chunk)
 
 
 def doubles(r_pairs, w_tiles, energy, shift, nb, nc):
@@ -497,6 +610,7 @@
             pltpu.SemaphoreType.DMA((3, chunks)),
             pltpu.SemaphoreType.DMA((3, chunks)),
             pltpu.SemaphoreType.DMA((6,)),
+            pltpu.SemaphoreType.DMA((2, chunks)),
             pltpu.SemaphoreType.DMA((3, steps)),
             pltpu.SemaphoreType.DMA((2, 6, 2 + nc // 2)),
             pltpu.SemaphoreType.DMA((2, 6, 3)),

time: 248 us -> 246 us (level)
  no operation moved by 1% of the time
where the time goes in v4:
time: 246 us; the launch traced here: 245 us
  Pallas kernels  243 us (99%)
    pallas_call x1, Pallas kernels, doubles(): pl.pallas_call(functools.partial(whole_kernel, nb, nc, chunks), out_shape...  243 us

profile of v4, /device:TPU:0, one launch (start us, length us, event | category | flops | bytes accessed | tf_op | source)
XLA Modules:
  0.0 245.4 jit_solution(14899831873380057135)
XLA Ops:
  0.7 243.2 %shard_map.46 = f32[3,64,128]{2,1,0:T(8,128)} custom-call(bf16[3,8,4,16,512]{4,3,2,1,0:T(8,128)(2,1)} %bitcast.3, bf16[1,3,64,128,512]{4,3,2,1,0:T(8,128)(2,1)} %refs_1_.1, f32[512]{0:T(512)} %refs_2_.1, f32[4,128]{1,0:T(4,128)} %bitcast.5, f32[1]{0:T(128)S(6)} %copy.6.refs_4_), custom_call_target="tpu_custom_call" | custom-call | tf_op jit(solution)/shard_map/pallas_call | solution.py:588
  243.8 1.5 copy.7

commit v5 on v4

--- a/solution.py
+++ b/solution.py
@@ -285,6 +285,11 @@
                     fetch_start(turn, unit + TURNS, steps - 1)
 
                 pair_up(unit).start()
+
+                @pl.when(unit > 0)
+                def _():
+                    pair_add(unit - 1)
+                    gather_in(unit - 1)
 
     stream = [(unit, tile) for unit in range(units) for tile in range(tiles) if tile * units + unit >= held]
 
@@ -538,10 +543,8 @@
     last_b_units()
     late_start()
 
-    @pl.loop(0, units)
-    def _(unit):
-        pair_add(unit)
-        gather_in(unit)
+    pair_add(units - 1)
+    gather_in(units - 1)
 
     widen_last_a()
 

time: 246 us -> 245 us (level)
  no operation moved by 1% of the time
where the time goes in v5:
time: 245 us; the launch traced here: 244 us
  Pallas kernels  242 us (99%)
    pallas_call x1, Pallas kernels, doubles(): pl.pallas_call(functools.partial(whole_kernel, nb, nc, chunks), out_shape...  242 us

profile of v5, /device:TPU:0, one launch (start us, length us, event | category | flops | bytes accessed | tf_op | source)
XLA Modules:
  0.0 244.5 jit_solution(5918659947665261002)
XLA Ops:
  0.7 242.2 %shard_map.46 = f32[3,64,128]{2,1,0:T(8,128)} custom-call(bf16[3,8,4,16,512]{4,3,2,1,0:T(8,128)(2,1)} %bitcast.3, bf16[1,3,64,128,512]{4,3,2,1,0:T(8,128)(2,1)} %refs_1_.1, f32[512]{0:T(512)} %refs_2_.1, f32[4,128]{1,0:T(4,128)} %bitcast.5, f32[1]{0:T(128)S(6)} %copy.6.refs_4_), custom_call_target="tpu_custom_call" | custom-call | tf_op jit(solution)/shard_map/pallas_call | solution.py:591
  242.9 1.5 copy.7
